TPU v7x, 512 devices: a whole 4x8x8 slice. The times are simulated.
512 devices in a mesh: tp: 16 (over z, core), ep: 32 (over y, x).
Axes of the slice: x: 4, y: 8, z: 8, core: 2. Of those that a mesh axis runs over, the one named last changes fastest.
Arguments:
- tokens: bfloat16 [12288, 2048], P('ep', 'tp'), may hold values from -6 to 6
- norm_gain: float32 [2048], replicated, may hold values from 0.25 to 1.75
- shared_gate: bfloat16 [2048, 2816], P('ep', 'tp'), may hold values from -0.125 to 0.125
- shared_up: bfloat16 [2048, 2816], P('ep', 'tp'), may hold values from -0.125 to 0.125
- shared_down: bfloat16 [2816, 2048], P('tp', 'ep'), may hold values from -0.21875 to 0.21875
- expert_gate: bfloat16 [16, 32, 176, 2048], P('tp', 'ep'), may hold values from -0.125 to 0.125
- expert_up: bfloat16 [16, 32, 176, 2048], P('tp', 'ep'), may hold values from -0.125 to 0.125
- expert_down: bfloat16 [64, 1408, 2048], P('ep', None, 'tp'), may hold values from -0.15625 to 0.15625
- chosen: int32 [64, 384], P('ep'), may hold values from 0 to 12287, as said below
- gates: float32 [64, 384], P('ep'), may hold values from 0.1 to 1
Outputs:
- mixed: bfloat16 [12288, 2048], P('ep', 'tp')
Inputs may be any that keep to these rules, and one draw needn't show every extreme that they name: Each row of chosen holds 384 different token indices in rising order. Of one row, at most 24 lie among the 384 tokens of one index of ep (tokens s * 384 to (s + 1) * 384 - 1), and in every row exactly 24 lie among those of some index.
All inputs are finite; a program needn't handle non-finite values.
Results may differ from a plain program's by a relative error of at most 0.012.
Values may be sent and summed in bfloat16 or wider, within the bound.
A program may use at most 64 MiB of HBM per device.

v0:
```python
import jax
import jax.numpy as jnp
from jax import lax
from jax.sharding import PartitionSpec as P

EXP_DEV = 2
TOK_DEV = 384
CAP = 384
norm_eps = 1e-06


def side_by_side(arrays, axis, dim, along):
    both = jnp.concatenate(arrays, axis=along)
    whole, at, gathered = (lax.all_gather(both, axis, axis=dim, tiled=True), 0, [])
    for a in arrays:
        gathered.append(lax.slice_in_dim(whole, at, at + a.shape[along], axis=along))
        at += a.shape[along]
    return tuple(gathered)


def sent_to_all(array, axis):
    length = lax.axis_size(axis)
    return lax.all_to_all(
        jnp.broadcast_to(array[None], (length, *array.shape)), axis, 0, 0, tiled=True
    )


def joined_along(pieces, dim):
    dims = list(pieces.shape[1:])
    dims[dim] *= pieces.shape[0]
    return jnp.moveaxis(pieces, 0, dim).reshape(dims)


def gathered_copies(array, axis, dim):
    pieces = sent_to_all(array, axis)
    return joined_along(pieces, dim)


def on_device(
    tokens,
    norm_gain,
    shared_gate,
    shared_up,
    shared_down,
    expert_gate,
    expert_up,
    expert_down,
    chosen,
    gates,
):
    tp_count = lax.axis_size("tp")
    ep_count = lax.axis_size("ep")
    slice_width = tokens.shape[1]
    whole = lax.all_gather(tokens, "tp", axis=1, tiled=True)
    widened = whole.astype(jnp.float32)
    inv_scale = lax.rsqrt(jnp.mean(widened * widened, axis=1, keepdims=True) + norm_eps)
    normed = (widened * inv_scale * norm_gain).astype(jnp.bfloat16)
    pieces = side_by_side((shared_gate, shared_up), "ep", 0, 1)
    gate_sum = jnp.dot(normed, pieces[0], preferred_element_type=jnp.float32)
    up_sum = jnp.dot(normed, pieces[1], preferred_element_type=jnp.float32)
    shared_hidden = (jax.nn.silu(gate_sum) * up_sum).astype(jnp.bfloat16)
    partial_out = jnp.dot(
        shared_hidden, gathered_copies(shared_down, "ep", 1), preferred_element_type=jnp.float32
    )
    shared_part = lax.psum_scatter(
        partial_out.astype(jnp.bfloat16), "tp", scatter_dimension=1, tiled=True
    ).astype(jnp.float32)
    slot_most = 2 * CAP // ep_count
    slot_count = ep_count * slot_most
    sources = chosen // TOK_DEV
    source_flags = (
        sources[:, :, None] == jnp.arange(ep_count, dtype=jnp.int32)[None, None, :]
    ).astype(jnp.int32)
    counts = jnp.sum(source_flags, axis=1)
    starts = jnp.cumsum(counts, axis=1) - counts
    run_start = jnp.take_along_axis(starts, sources, axis=1)
    slot_index = sources * slot_most + jnp.arange(CAP, dtype=jnp.int32)[None, :] - run_start
    local_ids = chosen - sources * TOK_DEV
    expert_rows = jnp.arange(EXP_DEV, dtype=jnp.int32)[:, None]
    requests = (
        jnp.full((EXP_DEV, slot_count), TOK_DEV, jnp.int32)
        .at[expert_rows, slot_index]
        .set(local_ids)
    )
    requests = requests.reshape(EXP_DEV, ep_count, slot_most)
    asked_ids = lax.all_to_all(requests, "ep", split_axis=1, concat_axis=1, tiled=True)
    clipped = jnp.minimum(asked_ids, TOK_DEV - 1)
    local_expert = lax.axis_index("tp") // (tp_count // EXP_DEV)
    own_requests = lax.dynamic_index_in_dim(clipped, local_expert, 0, keepdims=False)
    outgoing = jnp.take(normed, own_requests.reshape(-1), axis=0).reshape(ep_count, slot_most, -1)
    arrived = lax.all_to_all(outgoing, "ep", split_axis=0, concat_axis=0, tiled=True)
    token_rows = arrived.reshape(slot_count, -1)
    gate_weight = expert_gate.reshape(expert_gate.shape[2], expert_gate.shape[3])
    up_weight = expert_up.reshape(expert_up.shape[2], expert_up.shape[3])
    gate_values = jnp.einsum(
        "hd,rd->hr", gate_weight, token_rows, preferred_element_type=jnp.float32
    )
    up_values = jnp.einsum("hd,rd->hr", up_weight, token_rows, preferred_element_type=jnp.float32)
    part_hidden = (jax.nn.silu(gate_values) * up_values).astype(jnp.bfloat16)
    all_hidden = lax.all_gather(part_hidden, "tp", axis=0, tiled=True)
    width_hidden = expert_down.shape[1]
    placed_rows = []
    for expert_slot in range(EXP_DEV):
        hidden_block = all_hidden[expert_slot * width_hidden : (expert_slot + 1) * width_hidden, :]
        outputs = jnp.einsum(
            "fr,fd->rd", hidden_block, expert_down[expert_slot], preferred_element_type=jnp.float32
        )
        gate_slots = (
            jnp.zeros((slot_count,), jnp.float32)
            .at[slot_index[expert_slot]]
            .set(gates[expert_slot])
        )
        placed = (gate_slots[:, None] * outputs).astype(jnp.bfloat16)
        placed_rows.append(placed)
    stacked = jnp.stack(placed_rows).reshape(EXP_DEV, ep_count, slot_most, slice_width)
    returned = lax.all_to_all(stacked, "ep", split_axis=1, concat_axis=1, tiled=True)
    flat_values = returned.reshape(-1, slice_width)
    flat_ids = asked_ids.reshape(-1)
    picker = (jnp.arange(TOK_DEV, dtype=jnp.int32)[:, None] == flat_ids[None, :]).astype(
        jnp.bfloat16
    )
    routed = jnp.dot(picker, flat_values, preferred_element_type=jnp.float32)
    return (shared_part + routed).astype(jnp.bfloat16)


def solution(mesh):
    return jax.shard_map(
        on_device,
        mesh=mesh,
        in_specs=(
            P("ep", "tp"),
            P(),
            P("ep", "tp"),
            P("ep", "tp"),
            P("tp", "ep"),
            P("tp", "ep", None, None),
            P("tp", "ep", None, None),
            P("ep", None, "tp"),
            P("ep", None),
            P("ep", None),
        ),
        out_specs=P("ep", "tp"),
        check_vma=False,
    )
```

profile of v0, /device:TPU:4, one launch (start us, length us, event | category | flops | bytes accessed | tf_op | source)
XLA Modules:
  0.0 284.9 jit_solution(4781293270764742484)
XLA Ops:
  7.4 0.7 all-gather.4.cloned.1.call-update
  8.1 0.7 multiply_subtract_fusion
  8.8 0.1 convert_reduce_fusion
  8.9 0.2 reduce_window_sum.11
  9.2 6.6 %gather_fusion.1 = s32[768]{0:T(1024)S(1)} fusion(s32[2,32]{1,0:T(2,128)S(1)} %sub.20, s32[768]{0:T(1024)S(1)} %reshape.168), kind=kCustom, calls=%fused_computation.1 | custom fusion | bytes 12288 | tf_op jit(solution)/shard_map/jit(take_along_axis)/gather | solution.py:76
  15.9 36.5 %scatter_fusion = s32[2,768]{1,0:T(2,128)S(1)} fusion(s32[2,768]{1,0:T(2,128)S(1)} %broadcast_in_dim.23, s32[768]{0:T(1024)S(1)} %reshape.174, s32[768]{0:T(1024)S(1)} %reshape.176), kind=kCustom, calls=%fused_computation.2 | custom fusion | bytes 15360 | tf_op jit(solution)/shard_map/scatter | solution.py:83
  52.3 0.1 reshape.153
  52.4 0.6 copy.21
  53.1 10.2 %all-to-all-start.1 = ((s32[2,32,24]{2,0,1:T(2,128)}), s32[2,32,24]{2,0,1:T(2,128)S(1)}, u32[]{:S(2)}, u32[]{:S(2)}) async-start(s32[2,32,24]{2,0,1:T(2,128)} %copy.21), calls=%async_computation.1 | async-start | bytes 65536 | tf_op jit(solution)/shard_map/all_to_all | solution.py:86
  63.3 7.8 %all-to-all-done.1 = s32[2,32,24]{2,0,1:T(2,128)S(1)} async-done(((s32[2,32,24]{2,0,1:T(2,128)}), s32[2,32,24]{2,0,1:T(2,128)S(1)}, u32[]{:S(2)}, u32[]{:S(2)}) %all-to-all-start.1) | async-done | bytes 6176 | tf_op jit(solution)/shard_map/all_to_all | solution.py:86
  71.2 0.5 broadcast.160
  71.7 0.7 fusion.55
  72.4 0.1 reshape.155
  72.5 0.0 all-gather.4.cloned.1.call-done
  72.6 1.9 fusion
  74.5 0.4 fusion.2
  74.9 4.3 %gather_fusion = bf16[768,2048]{1,0:T(8,128)(2,1)} fusion(bf16[384,2048]{1,0:T(8,128)(2,1)S(1)} %fusion.2, s32[1024]{0:T(1024)S(1)} %pad_clamp_fusion), kind=kCustom, calls=%fused_computation | custom fusion | bytes 6294528 | tf_op jit(solution)/shard_map/jit(_take)/gather | solution.py:90
  79.2 3.9 %broadcast_select_fusion = bf16[32,24,2048]{2,1,0:T(8,128)(2,1)} fusion(bf16[32,24,2048]{2,1,0:T(8,128)(2,1)} %bitcast.63, pred[32,24]{1,0:T(8,128)(4,1)S(1)} %compare_and_fusion), kind=kLoop, calls=%fused_computation.10 | loop fusion | flops 1572864 | bytes 6292224 | tf_op jit(solution)/shard_map/jit(_take)/select_n | solution.py:90
  83.1 6.8 %all-to-all-start.2 = ((bf16[32,24,2048]{2,1,0:T(8,128)(2,1)}), bf16[32,24,2048]{2,1,0:T(8,128)(2,1)}, u32[]{:S(2)}, u32[]{:S(2)}) async-start(bf16[32,24,2048]{2,1,0:T(8,128)(2,1)} %broadcast_select_fusion), calls=%async_computation.2 | async-start | bytes 6291456 | tf_op jit(solution)/shard_map/all_to_all | solution.py:91
  89.9 0.0 all-gather.6.cloned.1.call-start
  90.0 0.7 pad_maximum_fusion.1
  90.7 0.0 all-gather.6.cloned.1.call-update
  90.7 0.0 all-gather.8.cloned.1.call-start
  90.8 73.0 %all-to-all-done.2 = bf16[32,24,2048]{2,1,0:T(8,128)(2,1)} async-done(((bf16[32,24,2048]{2,1,0:T(8,128)(2,1)}), bf16[32,24,2048]{2,1,0:T(8,128)(2,1)}, u32[]{:S(2)}, u32[]{:S(2)}) %all-to-all-start.2) | async-done | bytes 3145760 | tf_op jit(solution)/shard_map/all_to_all | solution.py:91
  163.8 3.2 %convolution_bitcast_fusion.1 = f32[176,768]{1,0:T(8,128)S(1)} fusion(bf16[768,2048]{1,0:T(8,128)(2,1)} %bitcast.7, bf16[1,1,176,2048]{3,2,1,0:T(8,128)(2,1)S(1)} %copy-done), kind=kOutput, calls=%fused_computation.19 | convolution fusion | flops 553648128 | bytes 4407296 | tf_op jit(solution)/shard_map/hd,rd->hr/dot_general | solution.py:95
  167.0 3.8 %fusion.9 = bf16[176,768]{1,0:T(8,128)(2,1)} fusion(bf16[768,2048]{1,0:T(8,128)(2,1)} %bitcast.7, bf16[1,1,176,2048]{3,2,1,0:T(8,128)(2,1)S(1)} %copy-done.8, f32[176,768]{1,0:T(8,128)S(1)} %convolution_bitcast_fusion.1), kind=kOutput, calls=%fused_computation.21 | convolution fusion | flops 554459136 | bytes 4677632 | tf_op jit(solution)/shard_map/hd,rd->hr/dot_general | solution.py:98
  170.8 0.0 all-gather.8.cloned.1.call-update
  170.9 1.1 broadcast_in_dim.19
  172.0 5.5 %all-to-all-start = ((bf16[32,176,64]{1,2,0:T(8,128)(2,1)}), bf16[32,176,64]{1,2,0:T(8,128)(2,1)S(1)}, u32[]{:S(2)}, u32[]{:S(2)}) async-start(bf16[32,176,64]{1,2,0:T(8,128)(2,1)} %broadcast_in_dim.19), calls=%async_computation | async-start | bytes 2097152 | tf_op jit(solution)/shard_map/all_to_all | solution.py:23
  177.5 0.0 reduce-scatter.4.cloned.1.call-start
  177.5 9.4 %all-gather.6.cloned.1.call-done = bf16[2048,352]{1,0:T(8,128)(2,1)} async-done(((bf16[64,352]{1,0:T(8,128)(2,1)}), bf16[2048,352]{1,0:T(8,128)(2,1)}) %all-gather.6.cloned.1.call-update) | async-done | bytes 1441808 | tf_op jit(solution)/shard_map/all_gather | solution.py:14
  186.9 2.6 fusion.28
  189.5 14.7 %all-to-all-done = bf16[32,176,64]{1,2,0:T(8,128)(2,1)S(1)} async-done(((bf16[32,176,64]{1,2,0:T(8,128)(2,1)}), bf16[32,176,64]{1,2,0:T(8,128)(2,1)S(1)}, u32[]{:S(2)}, u32[]{:S(2)}) %all-to-all-start) | async-done | bytes 720928 | tf_op jit(solution)/shard_map/all_to_all | solution.py:23
  204.2 4.3 %convolution_convert_fusion = bf16[384,2048]{1,0:T(8,128)(2,1)} fusion(bf16[176,2048]{0,1:T(8,128)(2,1)S(1)} %bitcast.65, bf16[384,2048]{1,0:T(8,128)(2,1)S(1)} %fusion.2, bf16[2048,352]{1,0:T(8,128)(2,1)} %all-gather.6.cloned.1.call-done, f32[384,176]{0,1:T(8,128)} %fusion.28), kind=kOutput, calls=%fused_computation.11 | convolution fusion | flops 554840064 | bytes 5185536 | tf_op jit(solution)/shard_map/dot_general | solution.py:62
  208.5 2.7 copy.26
  211.2 0.0 reduce-scatter.4.cloned.1.call-update
  211.3 3.1 %scatter_custom_fusion.1 = f32[768]{0:T(1024)S(1)} fusion(s32[384]{0:T(512)S(1)} %get-tuple-element.7, f32[384]{0:T(512)S(1)} %get-tuple-element.5, f32[]{:T(128)} %constant.48.clone.1), kind=kCustom, calls=%fused_computation.73 | custom fusion | bytes 3076 | tf_op jit(solution)/shard_map/scatter | solution.py:111
  214.4 2.9 %scatter_custom_fusion.2 = f32[768]{0:T(1024)S(1)} fusion(s32[384]{0:T(512)S(1)} %get-tuple-element.8, f32[384]{0:T(512)S(1)} %get-tuple-element.6, f32[]{:T(128)} %constant.48.clone.1), kind=kCustom, calls=%fused_computation.71 | custom fusion | bytes 3076 | tf_op jit(solution)/shard_map/scatter | solution.py:111
  217.3 16.4 %all-gather.8.cloned.1.call-done = bf16[2816,768]{1,0:T(8,128)(2,1)} async-done(((bf16[176,768]{1,0:T(8,128)(2,1)}), bf16[2816,768]{1,0:T(8,128)(2,1)}) %all-gather.8.cloned.1.call-update) | async-done | bytes 4325392 | tf_op jit(solution)/shard_map/all_gather | solution.py:100
  233.8 2.5 fusion.17
  236.3 0.3 copy-done.7
  236.7 0.8 fusion.20
  237.4 0.8 pad_maximum_fusion
  238.2 9.9 %all-to-all-start.3 = ((bf16[2,32,24,128]{3,2,0,1:T(8,128)(2,1)}), bf16[2,32,24,128]{3,2,0,1:T(8,128)(2,1)S(1)}, u32[]{:S(2)}, u32[]{:S(2)}) async-start(bf16[2,32,24,128]{3,2,0,1:T(8,128)(2,1)} %pad_maximum_fusion), calls=%async_computation.3 | async-start | bytes 786432 | tf_op jit(solution)/shard_map/all_to_all | solution.py:116
  248.1 0.1 eq.32
  248.2 27.1 %reduce-scatter.4.cloned.1.call-done = bf16[128,384]{1,0:T(8,128)(2,1)} async-done(((bf16[2048,384]{1,0:T(8,128)(2,1)}), bf16[128,384]{1,0:T(8,128)(2,1)}) %reduce-scatter.4.cloned.1.call-update) | async-done | bytes 98320
  275.3 1.0 copy.27
  276.3 1.2 fusion.25
  (37 shorter events, 0.2 us)
Async XLA Ops:
  7.4 156.5 %copy-start = (bf16[1,1,176,2048]{3,2,1,0:T(8,128)(2,1)S(1)}, bf16[1,1,176,2048]{3,2,1,0:T(8,128)(2,1)}, u32[]{:S(2)}) copy-start(bf16[1,1,176,2048]{3,2,1,0:T(8,128)(2,1)} %param.15) | copy-start | bytes 2162692
  7.4 65.2 %all-gather.4.cloned.1.call-start = ((), (), s32[]{:S(2)}) async-start(), calls=%async_computation.5 | async-start | bytes 1671168 | tf_op jit(solution)/shard_map/all_gather | solution.py:54
  15.8 58.6 %copy-start.5 = (f32[2048]{0:T(1024)S(1)}, f32[2048]{0:T(1024)}, u32[]{:S(2)}) copy-start(f32[2048]{0:T(1024)} %param.11) | copy-start | bytes 24580
  53.1 18.1 %all-to-all-start.1 = ((s32[2,32,24]{2,0,1:T(2,128)}), s32[2,32,24]{2,0,1:T(2,128)S(1)}, u32[]{:S(2)}, u32[]{:S(2)}) async-start(s32[2,32,24]{2,0,1:T(2,128)} %copy.21), calls=%async_computation.1 | async-start | bytes 65536 | tf_op jit(solution)/shard_map/all_to_all | solution.py:86
  72.6 1.9 copy-start.1
  83.1 6.9 %copy-start.2 = (bf16[64,176]{1,0:T(8,128)(2,1)S(1)}, bf16[64,176]{1,0:T(8,128)(2,1)}, u32[]{:S(2)}) copy-start(bf16[64,176]{1,0:T(8,128)(2,1)} %param.13) | copy-start | bytes 67588
  83.1 6.9 %copy-start.3 = (bf16[64,176]{1,0:T(8,128)(2,1)S(1)}, bf16[64,176]{1,0:T(8,128)(2,1)}, u32[]{:S(2)}) copy-start(bf16[64,176]{1,0:T(8,128)(2,1)} %param.12) | copy-start | bytes 67588
  83.1 80.7 %all-to-all-start.2 = ((bf16[32,24,2048]{2,1,0:T(8,128)(2,1)}), bf16[32,24,2048]{2,1,0:T(8,128)(2,1)}, u32[]{:S(2)}, u32[]{:S(2)}) async-start(bf16[32,24,2048]{2,1,0:T(8,128)(2,1)} %broadcast_select_fusion), calls=%async_computation.2 | async-start | bytes 6291456 | tf_op jit(solution)/shard_map/all_to_all | solution.py:91
  89.9 97.0 %all-gather.6.cloned.1.call-start = ((), (), s32[]{:S(2)}) async-start(), calls=%async_computation.6 | async-start | bytes 1622016 | tf_op jit(solution)/shard_map/all_gather | solution.py:14
  90.7 143.0 %all-gather.8.cloned.1.call-start = ((), (), s32[]{:S(2)}) async-start(), calls=%async_computation.7 | async-start | bytes 4595712 | tf_op jit(solution)/shard_map/all_gather | solution.py:100
  163.8 3.2 %copy-start.8 = (bf16[1,1,176,2048]{3,2,1,0:T(8,128)(2,1)S(1)}, bf16[1,1,176,2048]{3,2,1,0:T(8,128)(2,1)}, u32[]{:S(2)}) copy-start(bf16[1,1,176,2048]{3,2,1,0:T(8,128)(2,1)} %param.16) | copy-start | bytes 2162692
  167.0 3.8 %copy-start.4 = (bf16[176,64]{0,1:T(8,128)(2,1)S(1)}, bf16[176,64]{0,1:T(8,128)(2,1)}, u32[]{:S(2)}) copy-start(bf16[176,64]{0,1:T(8,128)(2,1)} %param.14) | copy-start | bytes 67588
  172.0 32.2 %all-to-all-start = ((bf16[32,176,64]{1,2,0:T(8,128)(2,1)}), bf16[32,176,64]{1,2,0:T(8,128)(2,1)S(1)}, u32[]{:S(2)}, u32[]{:S(2)}) async-start(bf16[32,176,64]{1,2,0:T(8,128)(2,1)} %broadcast_in_dim.19), calls=%async_computation | async-start | bytes 2097152 | tf_op jit(solution)/shard_map/all_to_all | solution.py:23
  177.5 97.8 %reduce-scatter.4.cloned.1.call-start = ((), (), s32[]{:S(2)}) async-start(), calls=%async_computation.8 | async-start | bytes 1671168
  208.5 2.7 copy-start.6
  208.5 25.3 %copy-start.9 = (bf16[2,1408,128]{2,1,0:T(8,128)(2,1)S(1)}, bf16[2,1408,128]{2,1,0:T(8,128)(2,1)}, u32[]{:S(2)}) copy-start(bf16[2,1408,128]{2,1,0:T(8,128)(2,1)} %param.17) | copy-start | bytes 2162692
  233.8 2.9 %copy-start.7 = (bf16[2816,768]{1,0:T(8,128)(2,1)S(1)}, bf16[2816,768]{1,0:T(8,128)(2,1)}, u32[]{:S(2)}) copy-start(bf16[2816,768]{1,0:T(8,128)(2,1)} %all-gather.8.cloned.1.call-done) | copy-start | bytes 12976132
  238.2 38.1 %all-to-all-start.3 = ((bf16[2,32,24,128]{3,2,0,1:T(8,128)(2,1)}), bf16[2,32,24,128]{3,2,0,1:T(8,128)(2,1)S(1)}, u32[]{:S(2)}, u32[]{:S(2)}) async-start(bf16[2,32,24,128]{3,2,0,1:T(8,128)(2,1)} %pad_maximum_fusion), calls=%async_computation.3 | async-start | bytes 786432 | tf_op jit(solution)/shard_map/all_to_all | solution.py:116
Sparse Core Ops, SparseCore 0:
  10.2 46.8 all-gather.3
  211.4 63.8 reduce-scatter.3
Sparse Core Ops, SparseCore 1:
  93.6 93.3 all-gather.5
  188.9 44.8 all-gather.7
where the time goes:
time: 286 us; the launch traced here: 285 us
  waiting for transfers between devices  149 us (52%)
  local copies, waits for them, and re-layouts  60.1 us (21%)
  starting transfers between devices  32.5 us (11%)
  matrix products  18.4 us (6%)
  between operations  15.2 us (5%)
  other arithmetic  9.57 us (3%)
    all_to_all x1, waiting for transfers between devices, on_device(): lax.all_to_all(outgoing, 'ep', split_axis=0, concat_axis=0, tiled=True)  73 us
    scatter x1, local copies, waits for them, and re-layouts, on_device(): requests = jnp.full((EXP_DEV, slot_count), TOK_DEV, jnp.int32).at[expert_...  36.5 us
    unnamed x5, waiting for transfers between devices  27.8 us
    all_gather x1, waiting for transfers between devices, on_device(): all_hidden = lax.all_gather(part_hidden, 'tp', axis=0, tiled=True)  16.4 us
    all_to_all x1, waiting for transfers between devices, sent_to_all(): lax.all_to_all(jnp.broadcast_to(array[None], (length, *array.shape)), axi...  14.7 us
    all_to_all x1, starting transfers between devices, on_device(): lax.all_to_all(requests, 'ep', split_axis=1, concat_axis=1, tiled=True)  10.2 us
    all_to_all x1, starting transfers between devices, on_device(): lax.all_to_all(stacked, 'ep', split_axis=1, concat_axis=1, tiled=True)  9.87 us
    all_gather x1, waiting for transfers between devices, side_by_side(): lax.all_gather(both, axis, axis=dim, tiled=True)  9.39 us
  transfers between devices with their start and end apart: 8, of which 6 were waited for; matrix products, arithmetic and copies ran while one was open for 27% of the time, Pallas kernels for 0%

commit v1 on v0

--- a/solution.py
+++ b/solution.py
@@ -97,7 +97,10 @@
     )
     up_values = jnp.einsum("hd,rd->hr", up_weight, token_rows, preferred_element_type=jnp.float32)
     part_hidden = (jax.nn.silu(gate_values) * up_values).astype(jnp.bfloat16)
-    all_hidden = lax.all_gather(part_hidden, "tp", axis=0, tiled=True)
+    pack_the_sites = lambda mine: jnp.concatenate(
+        lax.all_to_all(jnp.stack([mine] * lax.axis_size("tp")), "tp", 0, 0), axis=0
+    )
+    all_hidden = pack_the_sites(part_hidden)
     width_hidden = expert_down.shape[1]
     placed_rows = []
     for expert_slot in range(EXP_DEV):

time: 286 us -> 369 us (1.29)
  the two profiles are of different devices: /device:TPU:4 before, /device:TPU:2 now
where the time goes in v1:
time: 369 us
  waiting for transfers between devices  154 us (42%)
  blocking collectives  76.7 us (21%)
  local copies, waits for them, and re-layouts  65.4 us (18%)
  starting transfers between devices  34.1 us (9%)
  between operations  15.2 us (4%)
  matrix products  14.8 us (4%)
  other arithmetic  7.88 us (2%)
    all_gather x1, waiting for transfers between devices, side_by_side(): lax.all_gather(both, axis, axis=dim, tiled=True)  80.4 us
    all_to_all x1, blocking collectives, on_device(): lax.all_to_all(outgoing, 'ep', split_axis=0, concat_axis=0, tiled=True)  76.7 us
    unnamed x4, waiting for transfers between devices  43.8 us
    scatter x1, local copies, waits for them, and re-layouts, on_device(): requests = jnp.full((EXP_DEV, slot_count), TOK_DEV, jnp.int32).at[expert_...  36.5 us
    all_to_all x1, waiting for transfers between devices, sent_to_all(): lax.all_to_all(jnp.broadcast_to(array[None], (length, *array.shape)), axi...  21.3 us
    all_to_all x1, starting transfers between devices, on_device(): lax.all_to_all(jnp.stack([mine] * lax.axis_size('tp')), 'tp', 0, 0)  10.6 us
    all_to_all x1, starting transfers between devices, on_device(): lax.all_to_all(requests, 'ep', split_axis=1, concat_axis=1, tiled=True)  10.3 us
    all_to_all x1, waiting for transfers between devices, on_device(): lax.all_to_all(requests, 'ep', split_axis=1, concat_axis=1, tiled=True)  8.62 us
  transfers between devices with their start and end apart: 7, of which 5 were waited for; matrix products, arithmetic and copies ran while one was open for 20% of the time, Pallas kernels for 0%

profile of v1, /device:TPU:2, one launch (start us, length us, event | category | flops | bytes accessed | tf_op | source)
XLA Modules:
  0.0 368.6 jit_solution(2428803066650699998)
XLA Ops:
  7.4 0.7 all-gather.3.cloned.1.call-update
  8.1 0.7 multiply_subtract_fusion
  8.8 0.1 convert_reduce_fusion
  8.9 0.2 reduce_window_sum.11
  9.2 6.6 %gather_fusion.1 = s32[768]{0:T(1024)S(1)} fusion(s32[2,32]{1,0:T(2,128)S(1)} %sub.20, s32[768]{0:T(1024)S(1)} %reshape.173), kind=kCustom, calls=%fused_computation.1 | custom fusion | bytes 12288 | tf_op jit(solution)/shard_map/jit(take_along_axis)/gather | solution.py:76
  15.9 36.5 %scatter_fusion = s32[2,768]{1,0:T(2,128)S(1)} fusion(s32[2,768]{1,0:T(2,128)S(1)} %broadcast_in_dim.23, s32[768]{0:T(1024)S(1)} %reshape.179, s32[768]{0:T(1024)S(1)} %reshape.181), kind=kCustom, calls=%fused_computation.2 | custom fusion | bytes 15360 | tf_op jit(solution)/shard_map/scatter | solution.py:83
  52.3 0.1 reshape.158
  52.4 0.6 copy.21
  53.1 10.3 %all-to-all-start.1 = ((s32[2,32,24]{2,0,1:T(2,128)}), s32[2,32,24]{2,0,1:T(2,128)S(1)}, u32[]{:S(2)}, u32[]{:S(2)}) async-start(s32[2,32,24]{2,0,1:T(2,128)} %copy.21), calls=%async_computation.1 | async-start | bytes 65536 | tf_op jit(solution)/shard_map/all_to_all | solution.py:86
  63.4 8.6 %all-to-all-done.1 = s32[2,32,24]{2,0,1:T(2,128)S(1)} async-done(((s32[2,32,24]{2,0,1:T(2,128)}), s32[2,32,24]{2,0,1:T(2,128)S(1)}, u32[]{:S(2)}, u32[]{:S(2)}) %all-to-all-start.1) | async-done | bytes 6176 | tf_op jit(solution)/shard_map/all_to_all | solution.py:86
  72.0 0.5 broadcast.162
  72.5 0.7 fusion.41
  73.2 0.1 reshape.160
  73.4 0.0 all-gather.3.cloned.1.call-done
  73.4 1.9 fusion
  75.3 0.4 fusion.2
  75.8 4.3 %gather_fusion = bf16[768,2048]{1,0:T(8,128)(2,1)} fusion(bf16[384,2048]{1,0:T(8,128)(2,1)S(1)} %fusion.2, s32[1024]{0:T(1024)S(1)} %pad_clamp_fusion), kind=kCustom, calls=%fused_computation | custom fusion | bytes 6294528 | tf_op jit(solution)/shard_map/jit(_take)/gather | solution.py:90
  80.0 2.2 broadcast_select_fusion
  82.3 76.7 %all_to_all.25 = bf16[32,24,2048]{2,1,0:T(8,128)(2,1)} all-to-all(bf16[32,24,2048]{2,1,0:T(8,128)(2,1)S(1)} %broadcast_select_fusion), channel_id=1, replica_groups=mesh['tp'=16,'ep'=32] {'ep'}, dimensions={0} | all-to-all | bytes 6291456 | tf_op jit(solution)/shard_map/all_to_all | solution.py:91
  159.0 1.1 broadcast_in_dim.19
  160.1 5.6 %all-to-all-start = ((bf16[32,176,64]{1,2,0:T(8,128)(2,1)}), bf16[32,176,64]{1,2,0:T(8,128)(2,1)S(1)}, u32[]{:S(2)}, u32[]{:S(2)}) async-start(bf16[32,176,64]{1,2,0:T(8,128)(2,1)} %broadcast_in_dim.19), calls=%async_computation | async-start | bytes 2097152 | tf_op jit(solution)/shard_map/all_to_all | solution.py:23
  165.7 0.0 copy-start.8
  165.7 3.2 convolution_bitcast_fusion.1
  169.0 1.9 fusion.5
  170.9 21.3 %all-to-all-done = bf16[32,176,64]{1,2,0:T(8,128)(2,1)S(1)} async-done(((bf16[32,176,64]{1,2,0:T(8,128)(2,1)}), bf16[32,176,64]{1,2,0:T(8,128)(2,1)S(1)}, u32[]{:S(2)}, u32[]{:S(2)}) %all-to-all-start) | async-done | bytes 720928 | tf_op jit(solution)/shard_map/all_to_all | solution.py:23
  192.2 3.2 stack.8
  195.4 10.6 %all-to-all-start.3 = ((bf16[16,176,768]{2,1,0:T(8,128)(2,1)}), bf16[16,176,768]{2,1,0:T(8,128)(2,1)}, u32[]{:S(2)}, u32[]{:S(2)}) async-start(bf16[16,176,768]{2,1,0:T(8,128)(2,1)} %stack.8), calls=%async_computation.3 | async-start | bytes 8650752 | tf_op jit(solution)/shard_map/all_to_all | solution.py:101
  206.1 0.0 all-gather.5.cloned.1.call-start
  206.1 0.7 pad_maximum_fusion.1
  206.8 0.0 all-gather.5.cloned.1.call-update
  206.8 0.0 reduce-scatter.4.cloned.1.call-start
  206.9 80.4 %all-gather.5.cloned.1.call-done = bf16[2048,352]{1,0:T(8,128)(2,1)} async-done(((bf16[64,352]{1,0:T(8,128)(2,1)}), bf16[2048,352]{1,0:T(8,128)(2,1)}) %all-gather.5.cloned.1.call-update) | async-done | bytes 1441808 | tf_op jit(solution)/shard_map/all_gather | solution.py:14
  287.3 2.6 fusion.14
  289.9 4.3 %convolution_convert_fusion = bf16[384,2048]{1,0:T(8,128)(2,1)} fusion(bf16[176,2048]{0,1:T(8,128)(2,1)S(1)} %bitcast.73, bf16[384,2048]{1,0:T(8,128)(2,1)S(1)} %fusion.2, bf16[2048,352]{1,0:T(8,128)(2,1)} %all-gather.5.cloned.1.call-done, f32[384,176]{0,1:T(8,128)} %fusion.14), kind=kOutput, calls=%fused_computation.11 | convolution fusion | flops 554840064 | bytes 5185536 | tf_op jit(solution)/shard_map/dot_general | solution.py:62
  294.2 2.6 copy.26
  296.8 0.0 reduce-scatter.4.cloned.1.call-update
  296.9 3.1 scatter_custom_fusion.1
  300.0 2.9 scatter_custom_fusion.2
  303.0 0.2 all-to-all-done.3
  303.2 2.5 fusion.43
  305.8 0.8 fusion.7
  306.5 0.8 fusion.8
  307.3 0.8 pad_maximum_fusion
  308.1 7.6 %all-to-all-start.4 = ((bf16[2,32,24,128]{3,2,0,1:T(8,128)(2,1)}), bf16[2,32,24,128]{3,2,0,1:T(8,128)(2,1)S(1)}, u32[]{:S(2)}, u32[]{:S(2)}) async-start(bf16[2,32,24,128]{3,2,0,1:T(8,128)(2,1)} %pad_maximum_fusion), calls=%async_computation.4 | async-start | bytes 786432 | tf_op jit(solution)/shard_map/all_to_all | solution.py:119
  315.7 0.1 eq.32
  315.8 43.1 %reduce-scatter.4.cloned.1.call-done = bf16[128,384]{1,0:T(8,128)(2,1)} async-done(((bf16[2048,384]{1,0:T(8,128)(2,1)}), bf16[128,384]{1,0:T(8,128)(2,1)}) %reduce-scatter.4.cloned.1.call-update) | async-done | bytes 98320
  358.9 1.0 copy.27
  360.0 1.2 fusion.11
  (37 shorter events, 0.2 us)
Async XLA Ops:
  7.4 158.3 %copy-start = (bf16[1,1,176,2048]{3,2,1,0:T(8,128)(2,1)S(1)}, bf16[1,1,176,2048]{3,2,1,0:T(8,128)(2,1)}, u32[]{:S(2)}) copy-start(bf16[1,1,176,2048]{3,2,1,0:T(8,128)(2,1)} %param.15) | copy-start | bytes 2162692
  7.4 66.0 %all-gather.3.cloned.1.call-start = ((), (), s32[]{:S(2)}) async-start(), calls=%async_computation.6 | async-start | bytes 1671168 | tf_op jit(solution)/shard_map/all_gather | solution.py:54
  15.8 59.5 %copy-start.6 = (f32[2048]{0:T(1024)S(1)}, f32[2048]{0:T(1024)}, u32[]{:S(2)}) copy-start(f32[2048]{0:T(1024)} %param.11) | copy-start | bytes 24580
  53.1 18.9 %all-to-all-start.1 = ((s32[2,32,24]{2,0,1:T(2,128)}), s32[2,32,24]{2,0,1:T(2,128)S(1)}, u32[]{:S(2)}, u32[]{:S(2)}) async-start(s32[2,32,24]{2,0,1:T(2,128)} %copy.21), calls=%async_computation.1 | async-start | bytes 65536 | tf_op jit(solution)/shard_map/all_to_all | solution.py:86
  73.4 1.9 copy-start.1
  82.3 76.7 %copy-start.3 = (bf16[176,64]{0,1:T(8,128)(2,1)S(1)}, bf16[176,64]{0,1:T(8,128)(2,1)}, u32[]{:S(2)}) copy-start(bf16[176,64]{0,1:T(8,128)(2,1)} %param.14) | copy-start | bytes 67588
  160.1 32.1 %all-to-all-start = ((bf16[32,176,64]{1,2,0:T(8,128)(2,1)}), bf16[32,176,64]{1,2,0:T(8,128)(2,1)S(1)}, u32[]{:S(2)}, u32[]{:S(2)}) async-start(bf16[32,176,64]{1,2,0:T(8,128)(2,1)} %broadcast_in_dim.19), calls=%async_computation | async-start | bytes 2097152 | tf_op jit(solution)/shard_map/all_to_all | solution.py:23
  165.7 3.3 copy-start.2
  165.7 3.3 copy-start.8
  195.4 10.7 %copy-start.4 = (bf16[64,176]{1,0:T(8,128)(2,1)S(1)}, bf16[64,176]{1,0:T(8,128)(2,1)}, u32[]{:S(2)}) copy-start(bf16[64,176]{1,0:T(8,128)(2,1)} %param.13) | copy-start | bytes 67588
  195.4 10.7 %copy-start.5 = (bf16[64,176]{1,0:T(8,128)(2,1)S(1)}, bf16[64,176]{1,0:T(8,128)(2,1)}, u32[]{:S(2)}) copy-start(bf16[64,176]{1,0:T(8,128)(2,1)} %param.12) | copy-start | bytes 67588
  195.4 107.8 %all-to-all-start.3 = ((bf16[16,176,768]{2,1,0:T(8,128)(2,1)}), bf16[16,176,768]{2,1,0:T(8,128)(2,1)}, u32[]{:S(2)}, u32[]{:S(2)}) async-start(bf16[16,176,768]{2,1,0:T(8,128)(2,1)} %stack.8), calls=%async_computation.3 | async-start | bytes 8650752 | tf_op jit(solution)/shard_map/all_to_all | solution.py:101
  206.1 81.3 %all-gather.5.cloned.1.call-start = ((), (), s32[]{:S(2)}) async-start(), calls=%async_computation.7 | async-start | bytes 1622016 | tf_op jit(solution)/shard_map/all_gather | solution.py:14
  206.8 152.0 %reduce-scatter.4.cloned.1.call-start = ((), (), s32[]{:S(2)}) async-start(), calls=%async_computation.8 | async-start | bytes 1671168
  294.2 2.7 copy-start.7
  303.0 2.8 copy-start.9
  308.1 51.8 %all-to-all-start.4 = ((bf16[2,32,24,128]{3,2,0,1:T(8,128)(2,1)}), bf16[2,32,24,128]{3,2,0,1:T(8,128)(2,1)S(1)}, u32[]{:S(2)}, u32[]{:S(2)}) async-start(bf16[2,32,24,128]{3,2,0,1:T(8,128)(2,1)} %pad_maximum_fusion), calls=%async_computation.4 | async-start | bytes 786432 | tf_op jit(solution)/shard_map/all_to_all | solution.py:119
Sparse Core Ops, SparseCore 0:
  10.2 46.8 all-gather.2
  297.0 61.8 reduce-scatter.3
Sparse Core Ops, SparseCore 1:
  209.7 77.6 all-gather.4
